TPU v7x, 256 devices: a whole 4x4x8 slice. The times are simulated.
256 devices in a mesh: head: 8 (over x_hi, y), inner: 2 (over x_lo), outer: 16 (over z, core).
Axes of the slice: x: 4 (x_hi: 2, x_lo: 2; x = x_hi * 2 + x_lo), y: 4, z: 8, core: 2. Of those that a mesh axis runs over, the one named last changes fastest.
Arguments:
- query_nope: bfloat16 [4096, 8192], P(('inner', 'outer'), 'head'), may hold values from -6 to 6
- query_rope: bfloat16 [4096, 4096], P(('inner', 'outer'), 'head'), may hold values from -256 to 256
- latent: bfloat16 [4096, 512], P(('inner', 'outer')), may hold values from -6 to 6
- key_rope: bfloat16 [4096, 64], P(('inner', 'outer')), may hold values from -4 to 4
- key_up: bfloat16 [512, 8192], P(None, 'head'), may hold values from -0.25 to 0.25
- value_up: bfloat16 [512, 8192], P(None, 'head'), may hold values from -0.25 to 0.25
- latent_out: bfloat16 [4096, 32768], P(('inner', 'outer'), 'head'), may hold values from -3 to 3
- out_grad: bfloat16 [4096, 8192], P(('inner', 'outer'), 'head'), may hold values from -6 to 6
- logsum: float32 [4096, 64], P(('inner', 'outer'), 'head'), may hold values from 0 to 5000
- block_order: int32 [64], replicated, may hold values from 0 to 63, as said below
Outputs:
- d_query_nope: bfloat16 [4096, 8192], P(('inner', 'outer'), 'head')
- d_query_rope: bfloat16 [4096, 4096], P(('inner', 'outer'), 'head')
- d_latent: bfloat16 [4096, 512], P(('inner', 'outer'))
- d_key_rope: bfloat16 [4096, 64], P(('inner', 'outer'))
- d_key_up: float32 [512, 8192], P(('inner', 'outer'), 'head')
- d_value_up: float32 [512, 8192], P(('inner', 'outer'), 'head')
Inputs may be any that keep to these rules, and one draw needn't show every extreme that they name: `block_order`: stored blocks 2 r and 2 r + 1 hold sequence blocks c and 63 - c for some c, in either order; every sequence block is held once.
All inputs are finite; a program needn't handle non-finite values.
Results may differ from a plain program's by a relative error of at most 0.0085.
The roundings to bfloat16 on the way count: a program that leaves them out, or rounds other values in their place, can miss the bound.
Values may be sent and summed in bfloat16 or wider, within the bound.
No kernel may reach another device: no remote copies, remote signals or barrier semaphores. Data moves between devices by JAX's collectives and lax.ppermute only.
A program may use at most 128 MiB of HBM per device.

v0:
```python
import functools
import jax
import jax.numpy as jnp
from jax import lax
from jax.sharding import PartitionSpec as P

LATENT = 512
ROPE_DIM = 64
NOPE_DIM = 128
VALUE_DIM = 128


def split_up(shard, dim, count):
    shape = shard.shape
    pieces = shard.reshape(*shape[:dim], count, shape[dim] // count, *shape[dim + 1 :])
    return jnp.moveaxis(pieces, dim, 0)


def sum_packed(arrays, axis, dims):
    count = lax.axis_size(axis)
    pieces = [split_up(a, dim, count) for a, dim in zip(arrays, dims)]
    lines = jnp.concatenate([b.reshape(count, -1) for b in pieces], axis=1)
    width = max(16, -(-lines.shape[1] // 1024) * 8)
    lines = jnp.pad(lines, ((0, 0), (0, width * 128 - lines.shape[1]))).reshape(-1, 128)
    ravelled, at, gathered = (lax.psum_scatter(lines, axis, tiled=True).reshape(-1), 0, [])
    for b in pieces:
        part = b[0]
        gathered.append(ravelled[at : at + part.size].reshape(part.shape))
        at += part.size
    return tuple(gathered)


def sent_to_all(shard, axis):
    copies = jnp.broadcast_to(shard, (lax.axis_size(axis), *shard.shape))
    return lax.all_to_all(copies, axis, split_axis=0, concat_axis=0, tiled=True)


def of_everyone(shard, axis):
    everything = sent_to_all(shard, axis)
    return jnp.sum(everything, axis=0)


def in_one(arrays, axis):
    ends = [0]
    for a in arrays:
        ends.append(ends[-1] + a.size)
    subtotal = of_everyone(jnp.concatenate([a.ravel() for a in arrays]), axis)
    return tuple((subtotal[b:e].reshape(a.shape) for a, b, e in zip(arrays, ends, ends[1:])))


def side_by_side(arrays, axis, dim, along):
    ends, at = ([], 0)
    for a in arrays[:-1]:
        at += a.shape[along]
        ends.append(at)
    both = jnp.concatenate(arrays, axis=along)
    return tuple(
        jnp.split(lax.psum_scatter(both, axis, scatter_dimension=dim, tiled=True), ends, axis=along)
    )


def key_positions(block_order, first_row, length, block_size):
    indices = first_row + lax.iota(jnp.int32, length)
    owners = indices // block_size
    lookup = lax.iota(jnp.int32, block_order.shape[0])
    picked = (owners[:, None] == lookup[None, :]).astype(jnp.int32)
    return jnp.sum(picked * block_order[None, :], axis=1) * block_size + indices % block_size


def contract_last(first_op, second_op):
    return lax.dot_general(
        first_op, second_op, (((1,), (1,)), ((), ())), preferred_element_type=jnp.float32
    )


def contract_first(first_op, second_op):
    return lax.dot_general(
        first_op, second_op, (((0,), (0,)), ((), ())), preferred_element_type=jnp.float32
    )


def scaled_scores(queries, lat_keys, rope_keys):
    factor = float(NOPE_DIM + ROPE_DIM) ** (-0.5)
    return (contract_last(lat_keys, queries[0]) + contract_last(rope_keys, queries[1])) * factor


def unchanged(current):
    return current


def grad_update(carried, queries, lat_keys, rope_keys, positions):
    factor = float(NOPE_DIM + ROPE_DIM) ** (-0.5)
    scores = scaled_scores(queries, lat_keys, rope_keys)
    visible = positions[:, None] <= queries[2][None, :]
    weights = jnp.where(
        visible, jnp.exp(jnp.where(visible, scores - queries[5][None, :], 0.0)), 0.0
    )
    dprobs = contract_last(lat_keys, queries[3])
    dscore = (weights * (dprobs - queries[4][None, :]) * factor).astype(jnp.bfloat16)
    rounded = weights.astype(jnp.bfloat16)
    return (
        carried[0] + contract_first(dscore, lat_keys),
        carried[1] + contract_first(dscore, rope_keys),
        carried[2]
        + jnp.dot(dscore, queries[0], preferred_element_type=jnp.float32)
        + jnp.dot(rounded, queries[3], preferred_element_type=jnp.float32),
        carried[3] + jnp.dot(dscore, queries[1], preferred_element_type=jnp.float32),
    )


def single_block(carried, queries, lat_keys, rope_keys, positions, offset, block_size):
    part_lat = lax.dynamic_slice_in_dim(lat_keys, offset, block_size, 0)
    part_rope = lax.dynamic_slice_in_dim(rope_keys, offset, block_size, 0)
    part_pos = lax.dynamic_slice_in_dim(positions, offset, block_size, 0)
    sum_lat = lax.dynamic_slice_in_dim(carried[2], offset, block_size, 0)
    sum_rope = lax.dynamic_slice_in_dim(carried[3], offset, block_size, 0)
    result = grad_update(
        (carried[0], carried[1], sum_lat, sum_rope), queries, part_lat, part_rope, part_pos
    )
    return (
        result[0],
        result[1],
        lax.dynamic_update_slice_in_dim(carried[2], result[2], offset, 0),
        lax.dynamic_update_slice_in_dim(carried[3], result[3], offset, 0),
    )


def shard_grads(query_pairs, query_grads, lat_keys, rope_keys, positions):
    block_size = lat_keys.shape[0] // 2
    key_lat = jnp.zeros(lat_keys.shape, jnp.float32)
    key_rope_acc = jnp.zeros(rope_keys.shape, jnp.float32)
    updated = []
    for target in range(2):
        queries = query_pairs[target]
        latest = queries[2][-1]
        first_seen = positions[0] <= latest
        second_seen = positions[block_size] <= latest
        branch_index = first_seen.astype(jnp.int32) + second_seen.astype(jnp.int32)
        offset = jnp.where(first_seen, 0, block_size).astype(jnp.int32)
        whole = functools.partial(
            grad_update,
            queries=queries,
            lat_keys=lat_keys,
            rope_keys=rope_keys,
            positions=positions,
        )
        single = functools.partial(
            single_block,
            queries=queries,
            lat_keys=lat_keys,
            rope_keys=rope_keys,
            positions=positions,
            offset=offset,
            block_size=block_size,
        )
        carried = lax.switch(
            branch_index,
            [unchanged, single, whole],
            (query_grads[target][0], query_grads[target][1], key_lat, key_rope_acc),
        )
        updated.append((carried[0], carried[1]))
        key_lat, key_rope_acc = (carried[2], carried[3])
    return (tuple(updated), (key_lat, key_rope_acc))


def local(
    query_nope,
    query_rope,
    latent,
    key_rope,
    key_up,
    value_up,
    latent_out,
    out_grad,
    logsum,
    block_order,
):
    tokens = query_nope.shape[0]
    head_count = query_nope.shape[1] // NOPE_DIM
    block_size = tokens // 2
    flat_rows = block_size * head_count
    nope_heads = query_nope.reshape(tokens, head_count, NOPE_DIM)
    rope_heads = query_rope.reshape(tokens, head_count, ROPE_DIM)
    saved = latent_out.reshape(tokens, head_count, LATENT)
    upstream = out_grad.reshape(tokens, head_count, VALUE_DIM)
    key_map = key_up.reshape(LATENT, head_count, NOPE_DIM)
    value_map = value_up.reshape(LATENT, head_count, VALUE_DIM)
    query_latent = jnp.einsum(
        "thn,lhn->thl", nope_heads, key_map, preferred_element_type=jnp.float32
    ).astype(jnp.bfloat16)
    grad_latent = jnp.einsum(
        "thv,lhv->thl", upstream, value_map, preferred_element_type=jnp.float32
    ).astype(jnp.bfloat16)
    row_delta = jnp.sum(grad_latent.astype(jnp.float32) * saved.astype(jnp.float32), axis=2)
    context_size = lax.axis_size(("inner", "outer"))
    my_index = lax.axis_index(("inner", "outer"))
    own_positions = key_positions(block_order, my_index * tokens, tokens, block_size)
    query_parts = []
    for target in range(2):
        offset = target * block_size
        positions = jnp.broadcast_to(
            own_positions[offset : offset + block_size, None], (block_size, head_count)
        ).reshape(flat_rows)
        lat_part = query_latent[offset : offset + block_size].reshape(flat_rows, LATENT)
        rope_part = rope_heads[offset : offset + block_size].reshape(flat_rows, ROPE_DIM)
        grad_part = grad_latent[offset : offset + block_size].reshape(flat_rows, LATENT)
        delta_part = row_delta[offset : offset + block_size].reshape(flat_rows)
        total_part = logsum[offset : offset + block_size].reshape(flat_rows)
        query_parts.append((lat_part, rope_part, positions, grad_part, delta_part, total_part))
    backward_pairs = tuple(query_parts)
    zero_grads = tuple(
        (
            (
                jnp.zeros((flat_rows, LATENT), jnp.float32),
                jnp.zeros((flat_rows, ROPE_DIM), jnp.float32),
            )
            for target in range(2)
        )
    )
    every_lat, every_rope = (
        lax.all_gather(latent, ("inner", "outer"), axis=0, tiled=True),
        lax.all_gather(key_rope, ("inner", "outer"), axis=0, tiled=True),
    )

    def visit_pair(query_grads, turn_index):
        lat_rows = []
        rope_rows = []
        for member in range(2):
            shard_index = 2 * turn_index + member
            lat_keys = lax.dynamic_slice_in_dim(every_lat, shard_index * tokens, tokens, 0)
            rope_keys = lax.dynamic_slice_in_dim(every_rope, shard_index * tokens, tokens, 0)
            positions = key_positions(block_order, shard_index * tokens, tokens, block_size)
            query_grads, contribution = shard_grads(
                backward_pairs, query_grads, lat_keys, rope_keys, positions
            )
            lat_rows.append(contribution[0])
            rope_rows.append(contribution[1])
        return (query_grads, (jnp.stack(lat_rows), jnp.stack(rope_rows)))

    query_grads, stacked = lax.scan(visit_pair, zero_grads, lax.iota(jnp.int32, context_size // 2))
    all_lat = stacked[0].reshape(context_size * tokens, LATENT)
    all_rope = stacked[1].reshape(context_size * tokens, ROPE_DIM)
    own_sums = sum_packed((all_lat, all_rope), ("inner", "outer"), (0, 0))
    summed = in_one((own_sums[0], own_sums[1]), "head")
    grad_query = jnp.concatenate([query_grads[0][0], query_grads[1][0]], axis=0)
    grad_query = grad_query.reshape(tokens, head_count, LATENT).astype(jnp.bfloat16)
    grad_rope = jnp.concatenate([query_grads[0][1], query_grads[1][1]], axis=0)
    d_query_rope = grad_rope.reshape(tokens, head_count * ROPE_DIM).astype(jnp.bfloat16)
    d_query_nope = jnp.einsum(
        "thl,lhn->thn", grad_query, key_map, preferred_element_type=jnp.float32
    )
    d_query_nope = d_query_nope.reshape(tokens, head_count * NOPE_DIM).astype(jnp.bfloat16)
    key_weight = jnp.einsum(
        "thl,thn->lhn", grad_query, nope_heads, preferred_element_type=jnp.float32
    )
    value_weight = jnp.einsum("thl,thv->lhv", saved, upstream, preferred_element_type=jnp.float32)
    weight_parts = side_by_side(
        (
            key_weight.reshape(LATENT, head_count * NOPE_DIM),
            value_weight.reshape(LATENT, head_count * VALUE_DIM),
        ),
        ("inner", "outer"),
        0,
        1,
    )
    return (
        d_query_nope,
        d_query_rope,
        summed[0].astype(jnp.bfloat16),
        summed[1].astype(jnp.bfloat16),
        weight_parts[0],
        weight_parts[1],
    )


def solution(mesh):
    placed = (
        P(("inner", "outer"), "head"),
        P(("inner", "outer"), "head"),
        P(("inner", "outer"), None),
        P(("inner", "outer"), None),
        P(None, "head"),
        P(None, "head"),
        P(("inner", "outer"), "head"),
        P(("inner", "outer"), "head"),
        P(("inner", "outer"), "head"),
        P(),
    )
    return jax.shard_map(
        local,
        mesh=mesh,
        in_specs=placed,
        out_specs=(
            P(("inner", "outer"), "head"),
            P(("inner", "outer"), "head"),
            P(("inner", "outer"), None),
            P(("inner", "outer"), None),
            P(("inner", "outer"), "head"),
            P(("inner", "outer"), "head"),
        ),
        check_vma=False,
    )
```

profile of v0, /device:TPU:4, one launch (start us, length us, event | category | flops | bytes accessed | tf_op | source)
XLA Modules:
  0.0 1753.0 jit_solution(2727139085759418729)
XLA Ops:
  26.4 42.7 %all_gather.7 = bf16[4096,64]{1,0:T(8,128)(2,1)} all-gather(bf16[128,64]{1,0:T(8,128)(2,1)S(1)} %copy.107), channel_id=1, replica_groups=mesh['head'=8,'inner'=2,'outer'=16] {'inner','outer'}, dimensions={0}, use_global_device_ids=true | all-gather | bytes 540672 | tf_op jit(solution)/shard_map/all_gather | solution.py:222
  82.8 977.8 %while.24 = (s32[]{:T(128)}, f32[512,512]{1,0:T(8,128)S(1)}, f32[512,64]{0,1:T(8,128)}, f32[512,512]{1,0:T(8,128)}, f32[512,64]{0,1:T(8,128)}, /*index=5*/f32[16...) while((s32[]{:T(128)}, f32[512,512]{1,0:T(8,128)S(1)}, ...), condition=%wide.region_17.18_spmd.clone, body=%wide.region_2.17_spmd.clone.sunk | while | flops 1447517440 | bytes 55401404 | solution.py:240
  109.5 16.2 conditional.14
  129.4 14.1 conditional.13
  146.0 16.0 conditional.15
  223.7 14.0 conditional.12
  242.2 16.2 conditional.14
  355.0 16.1 conditional.14
  374.9 14.0 conditional.13
  391.4 15.9 conditional.15
  562.1 14.0 conditional.12
  580.5 16.1 conditional.14
  628.3 14.0 conditional.12
  646.8 16.1 conditional.14
  666.6 14.0 conditional.13
  683.1 15.9 conditional.15
  732.6 16.1 conditional.14
  780.4 14.0 conditional.12
  798.9 16.2 conditional.14
  911.9 14.1 conditional.13
  928.4 16.0 conditional.15
  978.1 16.1 conditional.14
  1105.4 511.1 %reduce-scatter.3.cloned.1.call-done = f32[576,128]{1,0:T(8,128)} async-done(((f32[18432,128]{1,0:T(8,128)}), f32[576,128]{1,0:T(8,128)}) %reduce-scatter.3.cloned.1.call-update) | async-done | bytes 294928 | tf_op jit(solution)/shard_map/reduce_scatter | solution.py:25
  1631.6 108.3 %reduce-scatter.5.cloned.1.call-done = f32[16,2048]{1,0:T(8,128)} async-done(((f32[512,2048]{1,0:T(8,128)}), f32[16,2048]{1,0:T(8,128)}) %reduce-scatter.5.cloned.1.call-update) | async-done | bytes 131088 | tf_op jit(solution)/shard_map/reduce_scatter | solution.py:58
  (1254 shorter events, 1152.0 us)
Async XLA Ops:
  7.2 72.5 %all-gather.2.cloned.1.call-start = ((), (), s32[]{:S(2)}) async-start(), calls=%async_computation.3 | async-start | bytes 4325376 | tf_op jit(solution)/shard_map/all_gather | solution.py:221
  7.9 1608.6 %reduce-scatter.3.cloned.1.call-start = ((), (), s32[]{:S(2)}) async-start(), calls=%async_computation.4 | async-start | bytes 9732096 | tf_op jit(solution)/shard_map/reduce_scatter | solution.py:25
  11.0 13.2 copy-start.45
  16.6 54.2 %copy-start.38 = (bf16[512,1024]{0,1:T(8,128)(2,1)}, bf16[512,1024]{0,1:T(8,128)(2,1)S(1)}, u32[]{:S(2)}) copy-start(bf16[512,1024]{0,1:T(8,128)(2,1)S(1)} %copy.139) | copy-start | bytes 3145732
  18.0 52.9 %copy-start.41 = (bf16[128,1024]{0,1:T(8,128)(2,1)}, bf16[128,1024]{0,1:T(8,128)(2,1)S(1)}, u32[]{:S(2)}) copy-start(bf16[128,1024]{0,1:T(8,128)(2,1)S(1)} %copy.140) | copy-start | bytes 786436
  129.4 16.6 copy-start.7
  195.7 12.8 copy-start.7
  262.1 12.8 copy-start.7
  308.6 12.8 copy-start.7
  374.9 16.5 copy-start.7
  441.0 12.8 copy-start.7
  487.5 12.8 copy-start.7
  534.1 12.8 copy-start.7
  600.3 12.8 copy-start.7
  666.6 16.5 copy-start.7
  752.4 12.8 copy-start.7
  818.9 12.8 copy-start.7
  865.4 12.8 copy-start.7
  911.9 16.6 copy-start.7
  997.9 12.8 copy-start.7
  1044.5 12.8 copy-start.7
  1091.7 648.3 %reduce-scatter.5.cloned.1.call-start = ((), (), s32[]{:S(2)}) async-start(), calls=%async_computation.5 | async-start | bytes 4325376 | tf_op jit(solution)/shard_map/reduce_scatter | solution.py:58
  1621.0 120.5 %all-to-all-start = ((f32[8,1,73728]{2,1,0:T(1,128)}), f32[8,1,73728]{2,1,0:T(1,128)}, u32[]{:S(2)}, u32[]{:S(2)}) async-start(f32[8,1,73728]{2,1,0:T(1,128)} %broadcast_in_dim.92), calls=%async_computation.1 | async-start | bytes 4718592 | tf_op jit(solution)/shard_map/all_to_all | solution.py:35
  1627.8 118.6 %copy-start.1 = (bf16[512,1024]{1,0:T(8,128)(2,1)S(1)}, bf16[512,1024]{1,0:T(8,128)(2,1)}, u32[]{:S(2)}) copy-start(bf16[512,1024]{1,0:T(8,128)(2,1)} %param.29) | copy-start | bytes 3145732
  (151 other events, 582.3 us)
Sparse Core Ops, SparseCore 0:
  9.9 69.7 all-gather.1
  1091.8 524.6 reduce-scatter.2
  1619.0 120.8 reduce-scatter.4
where the time goes:
time: 1790 us; the launch traced here: 1750 us
  waiting for transfers between devices  628 us (35%)
  matrix products  393 us (22%)
  local copies, waits for them, and re-layouts  383 us (21%)
  loops' own time  184 us (10%)
  other arithmetic  102 us (6%)
  blocking collectives  42.7 us (2%)
    reduce_scatter x1, waiting for transfers between devices, sum_packed(): lax.psum_scatter(lines, axis, tiled=True).reshape(-1)  511 us
    dot_general x132, matrix products, contract_last(): lax.dot_general(first_op, second_op, (((1,), (1,)), ((), ())), preferred_...  197 us
    another operation x1, loops' own time, local(): lax.scan(visit_pair, zero_grads, lax.iota(jnp.int32, context_size // 2))  179 us
    reduce_scatter x1, waiting for transfers between devices, side_by_side(): lax.psum_scatter(both, axis, scatter_dimension=dim, tiled=True)  108 us
    dot_general x44, matrix products, grad_update(): jnp.dot(rounded, queries[3], preferred_element_type=jnp.float32)  79.8 us
    dynamic_update_slice x32, other arithmetic, local(): lax.scan(visit_pair, zero_grads, lax.iota(jnp.int32, context_size // 2))  52.3 us
    dot_general x88, matrix products, contract_first(): lax.dot_general(first_op, second_op, (((0,), (0,)), ((), ())), preferred_...  50.4 us
    all_gather x1, blocking collectives, local(): lax.all_gather(key_rope, ('inner', 'outer'), axis=0, tiled=True)  42.7 us
  transfers between devices with their start and end apart: 4, of which 3 were waited for; matrix products, arithmetic and copies ran while one was open for 2% of the time, Pallas kernels for 0%

commit v1 on v0

--- a/solution.py
+++ b/solution.py
@@ -217,9 +217,18 @@
             for target in range(2)
         )
     )
+    apply_samples_all = lambda sheet: jnp.concatenate(
+        lax.all_to_all(
+            jnp.stack([sheet] * lax.axis_size(("inner", "outer")), axis=0),
+            ("inner", "outer"),
+            split_axis=0,
+            concat_axis=0,
+        ),
+        axis=0,
+    )
     every_lat, every_rope = (
         lax.all_gather(latent, ("inner", "outer"), axis=0, tiled=True),
-        lax.all_gather(key_rope, ("inner", "outer"), axis=0, tiled=True),
+        apply_samples_all(key_rope),
     )
 
     def visit_pair(query_grads, turn_index):

time: 1790 us -> 1800 us (level)
  blocking collectives: 42.7 us -> 0 us
  waiting for transfers between devices: 628 us -> 661 us
    all_gather x1 -> x0, blocking collectives: 42.7 us -> none  [local(): lax.all_gather(key_rope, ('inner', 'outer'), axis=0, tiled=True)]
    all_gather x1, waiting for transfers between devices: 7.51 us -> 39.7 us  [local(): lax.all_gather(latent, ('inner', 'outer'), axis=0, tiled=True)]
  transfers between devices with their start and end apart: 4 -> 5, of which waited for: 3 -> 4; matrix products, arithmetic and copies ran while one was open for 2% -> 3% of each run, Pallas kernels for 0% -> 0%
where the time goes in v1:
time: 1800 us; the launch traced here: 1760 us
  waiting for transfers between devices  661 us (37%)
  matrix products  394 us (22%)
  local copies, waits for them, and re-layouts  389 us (22%)
  loops' own time  186 us (10%)
  other arithmetic  101 us (6%)
    reduce_scatter x1, waiting for transfers between devices, sum_packed(): lax.psum_scatter(lines, axis, tiled=True).reshape(-1)  510 us
    dot_general x132, matrix products, contract_last(): lax.dot_general(first_op, second_op, (((1,), (1,)), ((), ())), preferred_...  197 us
    another operation x1, loops' own time, local(): lax.scan(visit_pair, zero_grads, lax.iota(jnp.int32, context_size // 2))  182 us
    reduce_scatter x1, waiting for transfers between devices, side_by_side(): lax.psum_scatter(both, axis, scatter_dimension=dim, tiled=True)  110 us
    dot_general x44, matrix products, grad_update(): jnp.dot(rounded, queries[3], preferred_element_type=jnp.float32)  80.2 us
    dynamic_update_slice x32, other arithmetic, local(): lax.scan(visit_pair, zero_grads, lax.iota(jnp.int32, context_size // 2))  52.5 us
    dot_general x88, matrix products, contract_first(): lax.dot_general(first_op, second_op, (((0,), (0,)), ((), ())), preferred_...  50.4 us
    slice x32, local copies, waits for them, and re-layouts, shard_grads(): latest = queries[2][-1]  41.1 us
  transfers between devices with their start and end apart: 5, of which 4 were waited for; matrix products, arithmetic and copies ran while one was open for 3% of the time, Pallas kernels for 0%

profile of v1, /device:TPU:4, one launch (start us, length us, event | category | flops | bytes accessed | tf_op | source)
XLA Modules:
  0.0 1763.4 jit_solution(15762667196714580868)
XLA Ops:
  42.9 39.7 %all-gather.2.cloned.1.call-done = bf16[4096,512]{1,0:T(8,128)(2,1)} async-done(((bf16[128,512]{1,0:T(8,128)(2,1)}), bf16[4096,512]{1,0:T(8,128)(2,1)}) %all-gather.2.cloned.1.call-update) | async-done | bytes 4194320 | tf_op jit(solution)/shard_map/all_gather | solution.py:230
  85.7 984.7 %while.24 = (s32[]{:T(128)}, f32[512,512]{1,0:T(8,128)S(1)}, f32[512,64]{0,1:T(8,128)}, f32[512,512]{1,0:T(8,128)}, f32[512,64]{0,1:T(8,128)}, /*index=5*/f32[16...) while((s32[]{:T(128)}, f32[512,512]{1,0:T(8,128)S(1)}, ...), condition=%wide.region_17.18_spmd.clone, body=%wide.region_2.17_spmd.clone.sunk | while | flops 1447517440 | bytes 55401404 | solution.py:249
  112.3 16.3 conditional.14
  132.5 14.2 conditional.13
  149.3 16.1 conditional.15
  227.4 14.1 conditional.12
  245.9 16.3 conditional.14
  359.6 16.2 conditional.14
  379.7 14.1 conditional.13
  396.5 16.0 conditional.15
  568.2 14.0 conditional.12
  586.6 16.2 conditional.14
  653.4 16.2 conditional.14
  673.5 14.1 conditional.13
  690.2 16.0 conditional.15
  739.8 16.2 conditional.14
  788.0 14.1 conditional.12
  806.6 16.3 conditional.14
  920.5 14.2 conditional.13
  937.3 16.1 conditional.15
  968.5 14.0 conditional.12
  987.0 16.2 conditional.14
  1116.8 510.1 %reduce-scatter.3.cloned.1.call-done = f32[576,128]{1,0:T(8,128)} async-done(((f32[18432,128]{1,0:T(8,128)}), f32[576,128]{1,0:T(8,128)}) %reduce-scatter.3.cloned.1.call-update) | async-done | bytes 294928 | tf_op jit(solution)/shard_map/reduce_scatter | solution.py:25
  1640.8 109.6 %reduce-scatter.5.cloned.1.call-done = f32[16,2048]{1,0:T(8,128)} async-done(((f32[512,2048]{1,0:T(8,128)}), f32[16,2048]{1,0:T(8,128)}) %reduce-scatter.5.cloned.1.call-update) | async-done | bytes 131088 | tf_op jit(solution)/shard_map/reduce_scatter | solution.py:58
  (1254 shorter events, 1163.2 us)
Async XLA Ops:
  7.2 22.2 %copy-start = (bf16[512,1024]{1,0:T(8,128)(2,1)S(1)}, bf16[512,1024]{1,0:T(8,128)(2,1)}, u32[]{:S(2)}) copy-start(bf16[512,1024]{1,0:T(8,128)(2,1)} %param.29) | copy-start | bytes 3145732
  7.2 15.1 copy-start.42
  7.2 75.4 %all-gather.2.cloned.1.call-start = ((), (), s32[]{:S(2)}) async-start(), calls=%async_computation.4 | async-start | bytes 4325376 | tf_op jit(solution)/shard_map/all_gather | solution.py:230
  9.6 31.0 %all-to-all-start = ((bf16[32,128,64]{1,2,0:T(8,128)(2,1)}), bf16[32,128,64]{1,2,0:T(8,128)(2,1)}, u32[]{:S(2)}, u32[]{:S(2)}) async-start(bf16[32,128,64]{1,2,0:T(8,128)(2,1)} %stack.101), calls=%async_computation | async-start | bytes 1048576 | tf_op jit(solution)/shard_map/all_to_all | solution.py:221
  19.2 1607.7 %reduce-scatter.3.cloned.1.call-start = ((), (), s32[]{:S(2)}) async-start(), calls=%async_computation.5 | async-start | bytes 9732096 | tf_op jit(solution)/shard_map/reduce_scatter | solution.py:25
  132.5 16.8 copy-start.7
  199.3 13.0 copy-start.7
  266.1 13.0 copy-start.7
  313.0 13.0 copy-start.7
  379.7 16.7 copy-start.7
  446.3 13.0 copy-start.7
  493.2 13.0 copy-start.7
  540.0 13.0 copy-start.7
  606.8 13.0 copy-start.7
  673.5 16.7 copy-start.7
  759.9 13.0 copy-start.7
  826.8 13.0 copy-start.7
  873.7 13.0 copy-start.7
  920.5 16.8 copy-start.7
  1007.1 13.0 copy-start.7
  1054.0 13.0 copy-start.7
  1101.5 648.9 %reduce-scatter.5.cloned.1.call-start = ((), (), s32[]{:S(2)}) async-start(), calls=%async_computation.6 | async-start | bytes 4325376 | tf_op jit(solution)/shard_map/reduce_scatter | solution.py:58
  1631.4 120.5 %all-to-all-start.1 = ((f32[8,1,73728]{2,1,0:T(1,128)}), f32[8,1,73728]{2,1,0:T(1,128)}, u32[]{:S(2)}, u32[]{:S(2)}) async-start(f32[8,1,73728]{2,1,0:T(1,128)} %broadcast_in_dim.92), calls=%async_computation.2 | async-start | bytes 4718592 | tf_op jit(solution)/shard_map/all_to_all | solution.py:35
  1638.2 118.6 %copy-start.1 = (bf16[512,1024]{1,0:T(8,128)(2,1)S(1)}, bf16[512,1024]{1,0:T(8,128)(2,1)}, u32[]{:S(2)}) copy-start(bf16[512,1024]{1,0:T(8,128)(2,1)} %param.29) | copy-start | bytes 3145732
  (151 other events, 603.0 us)
Sparse Core Ops, SparseCore 0:
  9.9 72.6 all-gather.1
  1101.6 525.2 reduce-scatter.2
  1629.4 120.8 reduce-scatter.4
